TPU v7x, 64 devices: a 2x2x8 block of a 4x4x8 slice. The times are simulated.
64 devices in a mesh: dp: 8 (over x, y, core), tp: 8 (over z).
Axes of the slice: x: 2, y: 2, z: 8, core: 2. Of those that a mesh axis runs over, the one named last changes fastest.
The devices are a block of a 4x4x8 slice.
Arguments:
- x: bfloat16 [14336, 5120], P(('dp', 'tp')), parts along dimension 0
- w_gate: bfloat16 [5120, 16384], P(None, 'tp')
- w_up: bfloat16 [5120, 16384], P(None, 'tp')
- w_down: bfloat16 [16384, 5120], P('tp')
Outputs:
- output: bfloat16 [14336, 5120], P(('dp', 'tp')), parts along dimension 0
There are 8 independent parts. A program takes and returns all parts, laid end to end along the dimension named above; an argument that names none is the same for every part.
All inputs are finite; a program needn't handle non-finite values.
Results may differ from a plain program's by a relative error of at most 0.016.
Values are sent between devices in bfloat16 or wider.
A program may use at most 768 MiB of HBM per device.

v0:
```python
import jax
import jax.numpy as jnp
from jax import lax
from jax.sharding import PartitionSpec as P


def solution(mesh):
    def step(x, w_gate, w_up, w_down):
        rows = lax.all_gather(x, "tp", axis=0, tiled=True)
        gate = jnp.dot(rows, w_gate, preferred_element_type=jnp.float32)
        up = jnp.dot(rows, w_up, preferred_element_type=jnp.float32)
        hidden = (jax.nn.silu(gate) * up).astype(jnp.bfloat16)
        term = jnp.dot(hidden, w_down, preferred_element_type=jnp.float32).astype(jnp.bfloat16)
        return lax.psum_scatter(term, "tp", scatter_dimension=0, tiled=True)

    return jax.shard_map(
        step,
        mesh=mesh,
        in_specs=(P(("dp", "tp"), None), P(None, "tp"), P(None, "tp"), P("tp", None)),
        out_specs=P(("dp", "tp"), None),
        check_vma=False,
    )
```

profile of v0, /device:TPU:21, one launch (start us, length us, event | category | flops | bytes accessed | tf_op | source)
XLA Modules:
  0.0 531.8 jit_solution(6870220047377135084)
XLA Ops:
  6.5 0.0 all-gather.2.cloned.1.call-start
  6.6 0.7 all-gather.2.cloned.1.call-update
  7.3 0.1 reduce-scatter.2.cloned.1.call-start
  7.4 190.1 %all-gather.2.cloned.1.call-done = bf16[1792,5120]{1,0:T(8,128)(2,1)} async-done(((bf16[224,5120]{1,0:T(8,128)(2,1)}), bf16[1792,5120]{1,0:T(8,128)(2,1)}) %all-gather.2.cloned.1.call-update) | async-done | bytes 18350096 | tf_op jit(solution)/shard_map/all_gather | solution.py:9
  197.4 46.9 %fusion = f32[1792,2048]{1,0:T(8,128)} fusion(bf16[1792,5120]{1,0:T(8,128)(2,1)} %all-gather.2.cloned.1.call-done, bf16[5120,2048]{1,0:T(8,128)(2,1)} %param.5), kind=kOutput, calls=%fused_computation.2 | convolution fusion | flops 37580963840 | bytes 54001664 | tf_op jit(solution)/shard_map/dot_general | solution.py:10
  244.3 51.4 %multiply_convert_fusion = bf16[1792,2048]{1,0:T(8,128)(2,1)} fusion(f32[1792,2048]{1,0:T(8,128)} %fusion, bf16[1792,5120]{1,0:T(8,128)(2,1)} %all-gather.2.cloned.1.call-done, bf16[5120,2048]{1,0:T(8,128)(2,1)} %param.6), kind=kOutput, calls=%fused_computation.1 | convolution fusion | flops 37602983936 | bytes 61341696 | tf_op jit(solution)/shard_map/dot_general | solution.py:11
  295.7 45.3 %convolution_convert_fusion = bf16[1792,5120]{1,0:T(8,128)(2,1)} fusion(bf16[1792,2048]{1,0:T(8,128)(2,1)} %multiply_convert_fusion, bf16[2048,5120]{1,0:T(8,128)(2,1)} %param.7), kind=kOutput, calls=%fused_computation | convolution fusion | flops 37590138880 | bytes 46661632 | tf_op jit(solution)/shard_map/dot_general | solution.py:13
  341.1 0.1 reduce-scatter.2.cloned.1.call-update
  341.1 183.8 %reduce-scatter.2.cloned.1.call-done = bf16[224,5120]{1,0:T(8,128)(2,1)} async-done(((bf16[1792,5120]{1,0:T(8,128)(2,1)}), bf16[224,5120]{1,0:T(8,128)(2,1)}) %reduce-scatter.2.cloned.1.call-update) | async-done | bytes 2293776 | tf_op jit(solution)/shard_map/reduce_scatter | solution.py:14
Async XLA Ops:
  6.5 190.9 %all-gather.2.cloned.1.call-start = ((), (), s32[]{:S(2)}) async-start(), calls=%async_computation.1 | async-start | bytes 20643840 | tf_op jit(solution)/shard_map/all_gather | solution.py:9
  7.3 517.6 %reduce-scatter.2.cloned.1.call-start = ((), (), s32[]{:S(2)}) async-start(), calls=%async_computation.2 | async-start | bytes 20643840 | tf_op jit(solution)/shard_map/reduce_scatter | solution.py:14
Sparse Core Ops, SparseCore 0:
  8.9 188.4 all-gather.1
  341.2 183.6 reduce-scatter.1
where the time goes:
time: 532 us
  waiting for transfers between devices  375 us (70%)
  matrix products  144 us (27%)
  between operations  13.4 us (3%)
    all_gather x1, waiting for transfers between devices, step(): rows = lax.all_gather(x, 'tp', axis=0, tiled=True)  190 us
    reduce_scatter x1, waiting for transfers between devices, step(): return lax.psum_scatter(term, 'tp', scatter_dimension=0, tiled=True)  184 us
    dot_general x1, matrix products, step(): up = jnp.dot(rows, w_up, preferred_element_type=jnp.float32)  51.4 us
    dot_general x1, matrix products, step(): gate = jnp.dot(rows, w_gate, preferred_element_type=jnp.float32)  46.9 us
    dot_general x1, matrix products, step(): jnp.dot(hidden, w_down, preferred_element_type=jnp.float32)  45.3 us
  transfers between devices with their start and end apart: 2, of which 2 were waited for; matrix products, arithmetic and copies ran while one was open for 0% of the time, Pallas kernels for 0%

commit v1 on v0

v1 whole, which is shorter than its diff:
```python
import functools

import jax
import jax.numpy as jnp
from jax import lax
from jax.experimental import pallas as pl
from jax.experimental.pallas import tpu as pltpu
from jax.sharding import PartitionSpec as P

MESH = pl.DeviceIdType.MESH
TILE_UP = 256
TILE_DOWN = 512
PIECE = 1024
DEPTH = 3
ORDER = (5, 7, 3, 6, 1, 4, 2)
AFTER = (None, None, 0, 1, 2, 3, 5)


def mlp_kernel(
    n, x_hbm, wg_hbm, wu_hbm, wd_hbm, y_hbm,
    xbuf, hid, rbuf, wbuf, dbuf,
    x_sem, w_sem, d_sem, y_sem, ag_send, ag_recv, rs_send, rs_recv,
):
    me = lax.axis_index("tp")
    peers = (lax.rem(me + 1, n), lax.rem(me + n - 1, n))
    rows, width = x_hbm.shape
    half = rows // 2
    units = xbuf.shape[0]
    sends = units - 1
    up_tiles = wg_hbm.shape[1] // TILE_UP
    down_tiles = width // TILE_DOWN
    pieces = width // PIECE
    per_piece = PIECE // TILE_DOWN
    top, bottom = pl.ds(0, half), pl.ds(half, half)

    def x_load(h):
        r = pl.ds(h * half, half)
        return pltpu.make_async_copy(x_hbm.at[r], xbuf.at[0, r], x_sem.at[h])

    def w_load(g):
        slot = lax.rem(g, DEPTH)
        cols = pl.ds(pl.multiple_of(lax.rem(g, up_tiles) * TILE_UP, TILE_UP), TILE_UP)
        return (
            pltpu.make_async_copy(wg_hbm.at[:, cols], wbuf.at[slot, :, pl.ds(0, TILE_UP)], w_sem.at[slot, 0]),
            pltpu.make_async_copy(wu_hbm.at[:, cols], wbuf.at[slot, :, pl.ds(TILE_UP, TILE_UP)], w_sem.at[slot, 1]),
        )

    def d_load(q):
        slot = lax.rem(q, DEPTH)
        cols = pl.ds(pl.multiple_of(lax.rem(q, down_tiles) * TILE_DOWN, TILE_DOWN), TILE_DOWN)
        return pltpu.make_async_copy(wd_hbm.at[:, cols], dbuf.at[slot], d_sem.at[slot])

    def gather_copy(k, d, src, dst_unit, dst_rows):
        return pltpu.make_async_remote_copy(
            src_ref=src,
            dst_ref=xbuf.at[dst_unit, dst_rows],
            send_sem=ag_send.at[d, k],
            recv_sem=ag_recv.at[d, k],
            device_id={"tp": peers[d]},
            device_id_type=MESH,
        )

    def sum_copy(r, d, p, src):
        rws = (bottom, top)[d]
        cols = pl.ds(pl.multiple_of(p * PIECE, PIECE), PIECE)
        return pltpu.make_async_remote_copy(
            src_ref=src.at[rws, cols],
            dst_ref=rbuf.at[r, rws, cols],
            send_sem=rs_send.at[d, r, p],
            recv_sem=rs_recv.at[d, r, p],
            device_id={"tp": peers[d]},
            device_id_type=MESH,
        )

    for h in (0, 1):
        x_load(h).start()
    for g in range(DEPTH - 1):
        for c in w_load(g):
            c.start()
    for q in range(DEPTH - 1):
        d_load(q).start()

    barrier = pltpu.get_barrier_semaphore()
    for d in (0, 1):
        pl.semaphore_signal(barrier, inc=1, device_id={"tp": peers[d]}, device_id_type=MESH)
    pl.semaphore_wait(barrier, 2)

    x_load(0).wait()
    gather_copy(0, 0, xbuf.at[0, top], 1, top).start()
    x_load(1).wait()
    gather_copy(0, 1, xbuf.at[0, bottom], 1, bottom).start()
    gather_copy(1, 0, xbuf.at[0, bottom], 2, top).start()
    gather_copy(1, 1, xbuf.at[0, top], 2, bottom).start()

    def hidden(j):
        def tile(t, carry):
            g = j * up_tiles + t
            for c in w_load(g):
                c.wait()

            @pl.when(g + DEPTH - 1 < units * up_tiles)
            def _():
                for c in w_load(g + DEPTH - 1):
                    c.start()

            both = jnp.dot(xbuf[j], wbuf[lax.rem(g, DEPTH)], preferred_element_type=jnp.float32)
            gate, up = both[:, :TILE_UP], both[:, TILE_UP:]
            out = gate * lax.logistic(gate) * up
            hid[j, :, pl.ds(pl.multiple_of(t * TILE_UP, TILE_UP), TILE_UP)] = out.astype(hid.dtype)
            return carry

        lax.fori_loop(0, up_tiles, tile, 0)

    def down(r, u, ready, finish, done):
        def piece(p, carry):
            ready(p)

            def tile(t, c2):
                i = p * per_piece + t
                q = r * down_tiles + i
                d_load(q).wait()

                @pl.when(q + DEPTH - 1 < units * down_tiles)
                def _():
                    d_load(q + DEPTH - 1).start()

                term = jnp.dot(hid[u], dbuf[lax.rem(q, DEPTH)], preferred_element_type=jnp.float32)
                finish(pl.ds(pl.multiple_of(i * TILE_DOWN, TILE_DOWN), TILE_DOWN), term)
                return c2

            lax.fori_loop(0, per_piece, tile, 0)
            done(p)
            return carry

        lax.fori_loop(0, pieces, piece, 0)

    def unit(j, carry):
        @pl.when((j >= 1) & (j < sends))
        def _():
            for d in (0, 1):
                gather_copy(j - 1, d, xbuf.at[0, (top, bottom)[d]], j, (top, bottom)[d]).wait_recv()

        @pl.when(j == sends)
        def _():
            for d in (0, 1):
                gather_copy(j - 1, d, xbuf.at[0, (bottom, top)[d]], j, (bottom, top)[d]).wait_recv()

        @pl.when((j >= 1) & (j < sends - 2))
        def _():
            for d in (0, 1):
                rws = (top, bottom)[d]
                gather_copy(j + 1, d, xbuf.at[j, rws], j + 2, rws).start()

        @pl.when(j == sends - 2)
        def _():
            for d in (0, 1):
                gather_copy(j + 1, d, xbuf.at[j, (top, bottom)[d]], j + 2, (bottom, top)[d]).start()

        hidden(j)

        @pl.when((j == sends - 2) | (j == sends))
        def _():
            r = (j - (sends - 2)) // 2
            for d in (0, 1):
                gather_copy(r + 2, d, xbuf.at[0, (top, bottom)[d]], 1, (top, bottom)[d]).wait_send()

            def finish(cols, term):
                xbuf[r + 1, :, cols] = term.astype(xbuf.dtype)

            def done(p):
                for d in (0, 1):
                    sum_copy(r, d, p, xbuf.at[r + 1]).start()

            down(r, j, lambda p: None, finish, done)

        return carry

    lax.fori_loop(0, units, unit, 0)

    def arrived(slots):
        def wait(p):
            for s in slots:
                for d in (0, 1):
                    sum_copy(s, d, p, rbuf.at[s]).wait_recv()

        return wait

    for r in range(2, sends):
        s = AFTER[r]

        def finish(cols, term, s=s):
            rbuf[s, :, cols] = (rbuf[s, :, cols].astype(jnp.float32) + term).astype(rbuf.dtype)

        def done(p, r=r, s=s):
            for d in (0, 1):
                sum_copy(r, d, p, rbuf.at[s]).start()

        down(r, ORDER[r], arrived((s,)), finish, done)

    for k in (0, 1, 4, 5, 6):
        for d in (0, 1):
            gather_copy(k, d, xbuf.at[0, top], 1, top).wait_send()

    def y_store(p):
        cols = pl.ds(pl.multiple_of(p * PIECE, PIECE), PIECE)
        return pltpu.make_async_copy(xbuf.at[0, :, cols], y_hbm.at[:, cols], y_sem.at[p])

    def finish(cols, term):
        for own, a, b in ((top, bottom, top), (bottom, top, bottom)):
            late = rbuf[6, a, cols].astype(jnp.float32)
            early = rbuf[4, b, cols].astype(jnp.float32)
            lo = 0 if own is top else half
            xbuf[0, own, cols] = (term[lo : lo + half] + early + late).astype(xbuf.dtype)

    down(units - 1, 0, arrived((4, 6)), finish, lambda p: y_store(p).start())

    def drain(p, carry):
        y_store(p).wait()
        for r in range(sends):
            for d in (0, 1):
                sum_copy(r, d, p, rbuf.at[0]).wait_send()
        return carry

    lax.fori_loop(0, pieces, drain, 0)


def solution(mesh):
    n = mesh.shape["tp"]

    def step(x, w_gate, w_up, w_down):
        rows, width = x.shape
        hidden = w_gate.shape[1]
        pieces = width // PIECE
        anywhere = pl.BlockSpec(memory_space=pl.ANY)
        return pl.pallas_call(
            functools.partial(mlp_kernel, n),
            out_shape=jax.ShapeDtypeStruct((rows, width), x.dtype),
            in_specs=[anywhere] * 4,
            out_specs=anywhere,
            scratch_shapes=[
                pltpu.VMEM((n, rows, width), x.dtype),
                pltpu.VMEM((n, rows, hidden), x.dtype),
                pltpu.VMEM((n - 1, rows, width), x.dtype),
                pltpu.VMEM((DEPTH, width, 2 * TILE_UP), x.dtype),
                pltpu.VMEM((DEPTH, hidden, TILE_DOWN), x.dtype),
                pltpu.SemaphoreType.DMA((2,)),
                pltpu.SemaphoreType.DMA((DEPTH, 2)),
                pltpu.SemaphoreType.DMA((DEPTH,)),
                pltpu.SemaphoreType.DMA((pieces,)),
                pltpu.SemaphoreType.DMA((2, n - 1)),
                pltpu.SemaphoreType.DMA((2, n - 1)),
                pltpu.SemaphoreType.DMA((2, n - 1, pieces)),
                pltpu.SemaphoreType.DMA((2, n - 1, pieces)),
            ],
            compiler_params=pltpu.CompilerParams(
                collective_id=0, has_side_effects=True, vmem_limit_bytes=67043328
            ),
            name="mlp_ring",
        )(x, w_gate, w_up, w_down)

    return jax.shard_map(
        step,
        mesh=mesh,
        in_specs=(P(("dp", "tp"), None), P(None, "tp"), P(None, "tp"), P("tp", None)),
        out_specs=P(("dp", "tp"), None),
        check_vma=False,
    )
```

time: 532 us -> 362 us (0.68)
  waiting for transfers between devices: 375 us -> 0 us
  Pallas kernels: 0 us -> 359 us
  matrix products: 144 us -> 0 us
  between operations: 13.4 us -> 0.01 us
    pallas_call x0 -> x1, Pallas kernels: none -> 359 us  [step(): pl.pallas_call(functools.partial(mlp_kernel, n), out_shape=jax.ShapeDtype...]
    all_gather x1 -> x0, waiting for transfers between devices: 190 us -> none  [step(): rows = lax.all_gather(x, 'tp', axis=0, tiled=True)]
    reduce_scatter x1 -> x0, waiting for transfers between devices: 184 us -> none  [step(): return lax.psum_scatter(term, 'tp', scatter_dimension=0, tiled=True)]
    dot_general x3 -> x0, matrix products: 144 us -> none  [the longest x1 51.4 us: step(): up = jnp.dot(rows, w_up, preferred_element_type=jnp.float32)]
  transfers between devices with their start and end apart: 2 -> 0, of which waited for: 2 -> 0; matrix products, arithmetic and copies ran while one was open for 0% -> 0% of each run, Pallas kernels for 0% -> 0%
where the time goes in v1:
time: 362 us
  Pallas kernels  359 us (99%)
    pallas_call x1, Pallas kernels, step(): pl.pallas_call(functools.partial(mlp_kernel, n), out_shape=jax.ShapeDtype...  359 us

profile of v1, /device:TPU:21, one launch (start us, length us, event | category | flops | bytes accessed | tf_op | source)
XLA Modules:
  0.0 362.2 jit_solution(3549847705763188133)
XLA Ops:
  0.0 359.0 %mlp_ring.1 = bf16[224,5120]{1,0:T(8,128)(2,1)} custom-call(bf16[224,5120]{1,0:T(8,128)(2,1)} %x_hbm.1, bf16[5120,2048]{1,0:T(8,128)(2,1)} %wg_hbm.1, bf16[5120,2048]{1,0:T(8,128)(2,1)} %wu_hbm.1, bf16[2048,5120]{1,0:T(8,128)(2,1)} %wd_hbm.1), custom_call_target="tpu_custom_call" | custom-call | tf_op jit(solution)/shard_map/mlp_ring/pallas_call | solution.py:235
  359.0 3.2 copy.6

commit v2 on v1

--- a/solution.py
+++ b/solution.py
@@ -12,14 +12,15 @@
 TILE_DOWN = 512
 PIECE = 1024
 DEPTH = 3
+KEPT = 4
 ORDER = (5, 7, 3, 6, 1, 4, 2)
 AFTER = (None, None, 0, 1, 2, 3, 5)
 
 
 def mlp_kernel(
-    n, x_hbm, wg_hbm, wu_hbm, wd_hbm, y_hbm,
-    xbuf, hid, rbuf, wbuf, dbuf,
-    x_sem, w_sem, d_sem, y_sem, ag_send, ag_recv, rs_send, rs_recv,
+    n, x_hbm, wg_hbm, wu_hbm, wd_hbm, y_ref,
+    xbuf, hid, rbuf, wbuf, dbuf, obuf,
+    x_sem, w_sem, d_sem, ag_send, ag_recv, rs_send, rs_recv,
 ):
     me = lax.axis_index("tp")
     peers = (lax.rem(me + 1, n), lax.rem(me + n - 1, n))
@@ -60,12 +61,15 @@
             device_id_type=MESH,
         )
 
-    def sum_copy(r, d, p, src):
+    def landing(r):
+        return rbuf.at[r] if r < KEPT else xbuf.at[r - 1]
+
+    def sum_copy(r, d, p, src, dst):
         rws = (bottom, top)[d]
         cols = pl.ds(pl.multiple_of(p * PIECE, PIECE), PIECE)
         return pltpu.make_async_remote_copy(
             src_ref=src.at[rws, cols],
-            dst_ref=rbuf.at[r, rws, cols],
+            dst_ref=dst.at[rws, cols],
             send_sem=rs_send.at[d, r, p],
             recv_sem=rs_recv.at[d, r, p],
             device_id={"tp": peers[d]},
@@ -169,59 +173,60 @@
 
             def done(p):
                 for d in (0, 1):
-                    sum_copy(r, d, p, xbuf.at[r + 1]).start()
+                    sum_copy(r, d, p, xbuf.at[r + 1], rbuf.at[r]).start()
 
             down(r, j, lambda p: None, finish, done)
 
         return carry
 
     lax.fori_loop(0, units, unit, 0)
-
-    def arrived(slots):
-        def wait(p):
-            for s in slots:
-                for d in (0, 1):
-                    sum_copy(s, d, p, rbuf.at[s]).wait_recv()
-
-        return wait
-
-    for r in range(2, sends):
-        s = AFTER[r]
-
-        def finish(cols, term, s=s):
-            rbuf[s, :, cols] = (rbuf[s, :, cols].astype(jnp.float32) + term).astype(rbuf.dtype)
-
-        def done(p, r=r, s=s):
-            for d in (0, 1):
-                sum_copy(r, d, p, rbuf.at[s]).start()
-
-        down(r, ORDER[r], arrived((s,)), finish, done)
 
     for k in (0, 1, 4, 5, 6):
         for d in (0, 1):
             gather_copy(k, d, xbuf.at[0, top], 1, top).wait_send()
 
-    def y_store(p):
+    def arrived(s, p):
+        for d in (0, 1):
+            sum_copy(s, d, p, landing(s), landing(s)).wait_recv()
+
+    for r in range(2, sends):
+        s = AFTER[r]
+
+        def finish(cols, term, s=s):
+            total = landing(s)
+            total[:, cols] = (total[:, cols].astype(jnp.float32) + term).astype(total.dtype)
+
+        def done(p, r=r, s=s):
+            for d in (0, 1):
+                sum_copy(r, d, p, landing(s), landing(r)).start()
+
+        down(r, ORDER[r], functools.partial(arrived, s), finish, done)
+
+    def left(lo, hi):
+        def drain(p, carry):
+            for r in range(lo, hi):
+                for d in (0, 1):
+                    sum_copy(r, d, p, landing(r), landing(r)).wait_send()
+            return carry
+
+        lax.fori_loop(0, pieces, drain, 0)
+
+    left(0, sends - 2)
+
+    early, late = landing(4), landing(6)
+
+    def finish(cols, term):
+        obuf[:, pl.ds(pl.multiple_of(lax.rem(cols.start, PIECE), TILE_DOWN), TILE_DOWN)] = term + early[:, cols].astype(jnp.float32)
+
+    def done(p):
+        arrived(6, p)
         cols = pl.ds(pl.multiple_of(p * PIECE, PIECE), PIECE)
-        return pltpu.make_async_copy(xbuf.at[0, :, cols], y_hbm.at[:, cols], y_sem.at[p])
-
-    def finish(cols, term):
-        for own, a, b in ((top, bottom, top), (bottom, top, bottom)):
-            late = rbuf[6, a, cols].astype(jnp.float32)
-            early = rbuf[4, b, cols].astype(jnp.float32)
-            lo = 0 if own is top else half
-            xbuf[0, own, cols] = (term[lo : lo + half] + early + late).astype(xbuf.dtype)
-
-    down(units - 1, 0, arrived((4, 6)), finish, lambda p: y_store(p).start())
-
-    def drain(p, carry):
-        y_store(p).wait()
-        for r in range(sends):
-            for d in (0, 1):
-                sum_copy(r, d, p, rbuf.at[0]).wait_send()
-        return carry
-
-    lax.fori_loop(0, pieces, drain, 0)
+        for own, other in ((top, bottom), (bottom, top)):
+            y_ref[own, cols] = (obuf[own, :] + late[other, cols].astype(jnp.float32)).astype(y_ref.dtype)
+
+    down(units - 1, 0, functools.partial(arrived, 4), finish, done)
+
+    left(sends - 2, sends)
 
 
 def solution(mesh):
@@ -234,26 +239,26 @@
         anywhere = pl.BlockSpec(memory_space=pl.ANY)
         return pl.pallas_call(
             functools.partial(mlp_kernel, n),
-            out_shape=jax.ShapeDtypeStruct((rows, width), x.dtype),
+            out_shape=pltpu.VMEM((rows, width), x.dtype),
             in_specs=[anywhere] * 4,
-            out_specs=anywhere,
+            out_specs=pl.BlockSpec(memory_space=pltpu.VMEM),
             scratch_shapes=[
                 pltpu.VMEM((n, rows, width), x.dtype),
                 pltpu.VMEM((n, rows, hidden), x.dtype),
-                pltpu.VMEM((n - 1, rows, width), x.dtype),
+                pltpu.VMEM((KEPT, rows, width), x.dtype),
                 pltpu.VMEM((DEPTH, width, 2 * TILE_UP), x.dtype),
                 pltpu.VMEM((DEPTH, hidden, TILE_DOWN), x.dtype),
+                pltpu.VMEM((rows, PIECE), jnp.float32),
                 pltpu.SemaphoreType.DMA((2,)),
                 pltpu.SemaphoreType.DMA((DEPTH, 2)),
                 pltpu.SemaphoreType.DMA((DEPTH,)),
-                pltpu.SemaphoreType.DMA((pieces,)),
                 pltpu.SemaphoreType.DMA((2, n - 1)),
                 pltpu.SemaphoreType.DMA((2, n - 1)),
                 pltpu.SemaphoreType.DMA((2, n - 1, pieces)),
                 pltpu.SemaphoreType.DMA((2, n - 1, pieces)),
             ],
             compiler_params=pltpu.CompilerParams(
-                collective_id=0, has_side_effects=True, vmem_limit_bytes=67043328
+                collective_id=0, has_side_effects=True, vmem_limit_bytes=62000000
             ),
             name="mlp_ring",
         )(x, w_gate, w_up, w_down)

time: 362 us -> 358 us (0.989)
  no operation moved by 1% of the time
where the time goes in v2:
time: 358 us
  Pallas kernels  357 us (100%)
    pallas_call x1, Pallas kernels, step(): pl.pallas_call(functools.partial(mlp_kernel, n), out_shape=pltpu.VMEM((ro...  357 us

profile of v2, /device:TPU:21, one launch (start us, length us, event | category | flops | bytes accessed | tf_op | source)
XLA Modules:
  0.0 358.3 jit_solution(2462118480639388599)
XLA Ops:
  0.0 356.9 %mlp_ring.1 = bf16[224,5120]{1,0:T(8,128)(2,1)S(1)} custom-call(bf16[224,5120]{1,0:T(8,128)(2,1)} %x_hbm.1, bf16[5120,2048]{1,0:T(8,128)(2,1)} %wg_hbm.1, bf16[5120,2048]{1,0:T(8,128)(2,1)} %wu_hbm.1, bf16[2048,5120]{1,0:T(8,128)(2,1)} %wd_hbm.1), custom_call_target="tpu_custom_call" | custom-call | tf_op jit(solution)/shard_map/mlp_ring/pallas_call | solution.py:240
  356.9 1.4 copy.6

commit v3 on v2

--- a/solution.py
+++ b/solution.py
@@ -15,12 +15,13 @@
 KEPT = 4
 ORDER = (5, 7, 3, 6, 1, 4, 2)
 AFTER = (None, None, 0, 1, 2, 3, 5)
+SPLIT = (0, 1, 5, 6)
 
 
 def mlp_kernel(
     n, x_hbm, wg_hbm, wu_hbm, wd_hbm, y_ref,
     xbuf, hid, rbuf, wbuf, dbuf, obuf,
-    x_sem, w_sem, d_sem, ag_send, ag_recv, rs_send, rs_recv,
+    x_sem, w_sem, d_sem, send_sem, ag_recv, rs_recv,
 ):
     me = lax.axis_index("tp")
     peers = (lax.rem(me + 1, n), lax.rem(me + n - 1, n))
@@ -31,6 +32,7 @@
     up_tiles = wg_hbm.shape[1] // TILE_UP
     down_tiles = width // TILE_DOWN
     pieces = width // PIECE
+    first = (0, pieces, 2 * pieces, 2 * pieces + 1, 2 * pieces + 2, pieces, 0)
     per_piece = PIECE // TILE_DOWN
     top, bottom = pl.ds(0, half), pl.ds(half, half)
 
@@ -42,9 +44,13 @@
         slot = lax.rem(g, DEPTH)
         cols = pl.ds(pl.multiple_of(lax.rem(g, up_tiles) * TILE_UP, TILE_UP), TILE_UP)
         return (
-            pltpu.make_async_copy(wg_hbm.at[:, cols], wbuf.at[slot, :, pl.ds(0, TILE_UP)], w_sem.at[slot, 0]),
-            pltpu.make_async_copy(wu_hbm.at[:, cols], wbuf.at[slot, :, pl.ds(TILE_UP, TILE_UP)], w_sem.at[slot, 1]),
-        )
+            pltpu.make_async_copy(wg_hbm.at[:, cols], wbuf.at[slot, :, pl.ds(0, TILE_UP)], w_sem.at[slot]),
+            pltpu.make_async_copy(wu_hbm.at[:, cols], wbuf.at[slot, :, pl.ds(TILE_UP, TILE_UP)], w_sem.at[slot]),
+        )
+
+    def w_wait(g):
+        slot = lax.rem(g, DEPTH)
+        pltpu.make_async_copy(wbuf.at[slot], wbuf.at[slot], w_sem.at[slot]).wait()
 
     def d_load(q):
         slot = lax.rem(q, DEPTH)
@@ -55,35 +61,39 @@
         return pltpu.make_async_remote_copy(
             src_ref=src,
             dst_ref=xbuf.at[dst_unit, dst_rows],
-            send_sem=ag_send.at[d, k],
-            recv_sem=ag_recv.at[d, k],
+            send_sem=send_sem.at[k],
+            recv_sem=ag_recv.at[d, lax.rem(k, ag_recv.shape[1])],
             device_id={"tp": peers[d]},
             device_id_type=MESH,
         )
 
-    def landing(r):
-        return rbuf.at[r] if r < KEPT else xbuf.at[r - 1]
-
-    def sum_copy(r, d, p, src, dst):
+    def sum_copy(r, base, d, p, src, dst):
         rws = (bottom, top)[d]
-        cols = pl.ds(pl.multiple_of(p * PIECE, PIECE), PIECE)
+        cols = pl.ds(0, width) if p is None else pl.ds(pl.multiple_of(p * PIECE, PIECE), PIECE)
         return pltpu.make_async_remote_copy(
             src_ref=src.at[rws, cols],
             dst_ref=dst.at[rws, cols],
-            send_sem=rs_send.at[d, r, p],
-            recv_sem=rs_recv.at[d, r, p],
+            send_sem=send_sem.at[lax.rem(r + 2, sends)],
+            recv_sem=rs_recv.at[d, base if p is None else base + p],
             device_id={"tp": peers[d]},
             device_id_type=MESH,
         )
 
+    def landing(r):
+        return rbuf.at[r] if r < KEPT else xbuf.at[r - 1]
+
+    def left(k):
+        pltpu.make_async_remote_copy(
+            src_ref=xbuf.at[0],
+            dst_ref=xbuf.at[0],
+            send_sem=send_sem.at[k],
+            recv_sem=ag_recv.at[0, 0],
+            device_id={"tp": peers[0]},
+            device_id_type=MESH,
+        ).wait_send()
+
     for h in (0, 1):
         x_load(h).start()
-    for g in range(DEPTH - 1):
-        for c in w_load(g):
-            c.start()
-    for q in range(DEPTH - 1):
-        d_load(q).start()
-
     barrier = pltpu.get_barrier_semaphore()
     for d in (0, 1):
         pl.semaphore_signal(barrier, inc=1, device_id={"tp": peers[d]}, device_id_type=MESH)
@@ -95,12 +105,19 @@
     gather_copy(0, 1, xbuf.at[0, bottom], 1, bottom).start()
     gather_copy(1, 0, xbuf.at[0, bottom], 2, top).start()
     gather_copy(1, 1, xbuf.at[0, top], 2, bottom).start()
+    for g in range(DEPTH - 1):
+        for c in w_load(g):
+            c.start()
+    for q in range(DEPTH - 1):
+        d_load(q).start()
+
+    def nothing(p):
+        return None
 
     def hidden(j):
         def tile(t, carry):
             g = j * up_tiles + t
-            for c in w_load(g):
-                c.wait()
+            w_wait(g)
 
             @pl.when(g + DEPTH - 1 < units * up_tiles)
             def _():
@@ -165,29 +182,31 @@
         @pl.when((j == sends - 2) | (j == sends))
         def _():
             r = (j - (sends - 2)) // 2
-            for d in (0, 1):
-                gather_copy(r + 2, d, xbuf.at[0, (top, bottom)[d]], 1, (top, bottom)[d]).wait_send()
+            left(r + 2)
 
             def finish(cols, term):
                 xbuf[r + 1, :, cols] = term.astype(xbuf.dtype)
 
             def done(p):
                 for d in (0, 1):
-                    sum_copy(r, d, p, xbuf.at[r + 1], rbuf.at[r]).start()
-
-            down(r, j, lambda p: None, finish, done)
+                    sum_copy(r, r * pieces, d, p, xbuf.at[r + 1], rbuf.at[r]).start()
+
+            down(r, j, nothing, finish, done)
 
         return carry
 
     lax.fori_loop(0, units, unit, 0)
 
-    for k in (0, 1, 4, 5, 6):
-        for d in (0, 1):
-            gather_copy(k, d, xbuf.at[0, top], 1, top).wait_send()
+    for k in (4, 5, 6, 0, 1):
+        left(k)
 
     def arrived(s, p):
         for d in (0, 1):
-            sum_copy(s, d, p, landing(s), landing(s)).wait_recv()
+            sum_copy(s, first[s], d, p, landing(s), landing(s)).wait_recv()
+
+    def send(r, p):
+        for d in (0, 1):
+            sum_copy(r, first[r], d, p, landing(AFTER[r]), landing(r)).start()
 
     for r in range(2, sends):
         s = AFTER[r]
@@ -196,27 +215,26 @@
             total = landing(s)
             total[:, cols] = (total[:, cols].astype(jnp.float32) + term).astype(total.dtype)
 
-        def done(p, r=r, s=s):
-            for d in (0, 1):
-                sum_copy(r, d, p, landing(s), landing(r)).start()
-
-        down(r, ORDER[r], functools.partial(arrived, s), finish, done)
-
-    def left(lo, hi):
-        def drain(p, carry):
-            for r in range(lo, hi):
-                for d in (0, 1):
-                    sum_copy(r, d, p, landing(r), landing(r)).wait_send()
-            return carry
-
-        lax.fori_loop(0, pieces, drain, 0)
-
-    left(0, sends - 2)
+        if s not in SPLIT:
+            arrived(s, None)
+        down(
+            r,
+            ORDER[r],
+            functools.partial(arrived, s) if s in SPLIT else nothing,
+            finish,
+            functools.partial(send, r) if r in SPLIT else nothing,
+        )
+        if r not in SPLIT:
+            send(r, None)
+
+    for r in range(sends - 2):
+        left((r + 2) % sends)
 
     early, late = landing(4), landing(6)
 
     def finish(cols, term):
-        obuf[:, pl.ds(pl.multiple_of(lax.rem(cols.start, PIECE), TILE_DOWN), TILE_DOWN)] = term + early[:, cols].astype(jnp.float32)
+        within = pl.ds(pl.multiple_of(lax.rem(cols.start, PIECE), TILE_DOWN), TILE_DOWN)
+        obuf[:, within] = term + early[:, cols].astype(jnp.float32)
 
     def done(p):
         arrived(6, p)
@@ -224,9 +242,10 @@
         for own, other in ((top, bottom), (bottom, top)):
             y_ref[own, cols] = (obuf[own, :] + late[other, cols].astype(jnp.float32)).astype(y_ref.dtype)
 
-    down(units - 1, 0, functools.partial(arrived, 4), finish, done)
-
-    left(sends - 2, sends)
+    arrived(4, None)
+    down(units - 1, 0, nothing, finish, done)
+    for r in (sends - 2, sends - 1):
+        left((r + 2) % sends)
 
 
 def solution(mesh):
@@ -235,7 +254,6 @@
     def step(x, w_gate, w_up, w_down):
         rows, width = x.shape
         hidden = w_gate.shape[1]
-        pieces = width // PIECE
         anywhere = pl.BlockSpec(memory_space=pl.ANY)
         return pl.pallas_call(
             functools.partial(mlp_kernel, n),
@@ -250,12 +268,11 @@
                 pltpu.VMEM((DEPTH, hidden, TILE_DOWN), x.dtype),
                 pltpu.VMEM((rows, PIECE), jnp.float32),
                 pltpu.SemaphoreType.DMA((2,)),
-                pltpu.SemaphoreType.DMA((DEPTH, 2)),
                 pltpu.SemaphoreType.DMA((DEPTH,)),
-                pltpu.SemaphoreType.DMA((2, n - 1)),
-                pltpu.SemaphoreType.DMA((2, n - 1)),
-                pltpu.SemaphoreType.DMA((2, n - 1, pieces)),
-                pltpu.SemaphoreType.DMA((2, n - 1, pieces)),
+                pltpu.SemaphoreType.DMA((DEPTH,)),
+                pltpu.SemaphoreType.DMA((n - 1,)),
+                pltpu.SemaphoreType.DMA((2, n // 2)),
+                pltpu.SemaphoreType.DMA((2, 2 * (width // PIECE) + 3)),
             ],
             compiler_params=pltpu.CompilerParams(
                 collective_id=0, has_side_effects=True, vmem_limit_bytes=62000000

time: 358 us -> 356 us (level)
  no operation moved by 1% of the time
where the time goes in v3:
time: 356 us
  Pallas kernels  354 us (99%)
    pallas_call x1, Pallas kernels, step(): pl.pallas_call(functools.partial(mlp_kernel, n), out_shape=pltpu.VMEM((ro...  354 us

profile of v3, /device:TPU:21, one launch (start us, length us, event | category | flops | bytes accessed | tf_op | source)
XLA Modules:
  0.0 355.5 jit_solution(14513311723715911895)
XLA Ops:
  0.0 354.1 %mlp_ring.1 = bf16[224,5120]{1,0:T(8,128)(2,1)S(1)} custom-call(bf16[224,5120]{1,0:T(8,128)(2,1)} %x_hbm.1, bf16[5120,2048]{1,0:T(8,128)(2,1)} %wg_hbm.1, bf16[5120,2048]{1,0:T(8,128)(2,1)} %wu_hbm.1, bf16[2048,5120]{1,0:T(8,128)(2,1)} %wd_hbm.1), custom_call_target="tpu_custom_call" | custom-call | tf_op jit(solution)/shard_map/mlp_ring/pallas_call | solution.py:258
  354.1 1.4 copy.6

commit v4 on v3

--- a/solution.py
+++ b/solution.py
@@ -12,6 +12,7 @@
 TILE_DOWN = 512
 PIECE = 1024
 DEPTH = 3
+HEAD = 48
 KEPT = 4
 ORDER = (5, 7, 3, 6, 1, 4, 2)
 AFTER = (None, None, 0, 1, 2, 3, 5)
@@ -32,13 +33,13 @@
     up_tiles = wg_hbm.shape[1] // TILE_UP
     down_tiles = width // TILE_DOWN
     pieces = width // PIECE
-    first = (0, pieces, 2 * pieces, 2 * pieces + 1, 2 * pieces + 2, pieces, 0)
+    first = (0, pieces, 0, 1, 3, pieces, 0)
     per_piece = PIECE // TILE_DOWN
     top, bottom = pl.ds(0, half), pl.ds(half, half)
 
-    def x_load(h):
-        r = pl.ds(h * half, half)
-        return pltpu.make_async_copy(x_hbm.at[r], xbuf.at[0, r], x_sem.at[h])
+    def x_load(h, part):
+        rws = pl.ds(h * half + (0, HEAD)[part], (HEAD, half - HEAD)[part])
+        return pltpu.make_async_copy(x_hbm.at[rws], xbuf.at[0, rws], x_sem.at[h, part])
 
     def w_load(g):
         slot = lax.rem(g, DEPTH)
@@ -74,7 +75,7 @@
             src_ref=src.at[rws, cols],
             dst_ref=dst.at[rws, cols],
             send_sem=send_sem.at[lax.rem(r + 2, sends)],
-            recv_sem=rs_recv.at[d, base if p is None else base + p],
+            recv_sem=ag_recv.at[d, base] if p is None else rs_recv.at[d, base + p],
             device_id={"tp": peers[d]},
             device_id_type=MESH,
         )
@@ -92,17 +93,19 @@
             device_id_type=MESH,
         ).wait_send()
 
-    for h in (0, 1):
-        x_load(h).start()
     barrier = pltpu.get_barrier_semaphore()
     for d in (0, 1):
         pl.semaphore_signal(barrier, inc=1, device_id={"tp": peers[d]}, device_id_type=MESH)
+    for part in (0, 1):
+        for h in (0, 1):
+            x_load(h, part).start()
     pl.semaphore_wait(barrier, 2)
 
-    x_load(0).wait()
-    gather_copy(0, 0, xbuf.at[0, top], 1, top).start()
-    x_load(1).wait()
-    gather_copy(0, 1, xbuf.at[0, bottom], 1, bottom).start()
+    for part in (0, 1):
+        for d in (0, 1):
+            x_load(d, part).wait()
+            rws = pl.ds(d * half + (0, HEAD)[part], (HEAD, half - HEAD)[part])
+            gather_copy(0, d, xbuf.at[0, rws], 1, rws).start()
     gather_copy(1, 0, xbuf.at[0, bottom], 2, top).start()
     gather_copy(1, 1, xbuf.at[0, top], 2, bottom).start()
     for g in range(DEPTH - 1):
@@ -267,12 +270,12 @@
                 pltpu.VMEM((DEPTH, width, 2 * TILE_UP), x.dtype),
                 pltpu.VMEM((DEPTH, hidden, TILE_DOWN), x.dtype),
                 pltpu.VMEM((rows, PIECE), jnp.float32),
-                pltpu.SemaphoreType.DMA((2,)),
+                pltpu.SemaphoreType.DMA((2, 2)),
                 pltpu.SemaphoreType.DMA((DEPTH,)),
                 pltpu.SemaphoreType.DMA((DEPTH,)),
                 pltpu.SemaphoreType.DMA((n - 1,)),
                 pltpu.SemaphoreType.DMA((2, n // 2)),
-                pltpu.SemaphoreType.DMA((2, 2 * (width // PIECE) + 3)),
+                pltpu.SemaphoreType.DMA((2, 2 * (width // PIECE))),
             ],
             compiler_params=pltpu.CompilerParams(
                 collective_id=0, has_side_effects=True, vmem_limit_bytes=62000000

time: 356 us -> 355 us (level)
  no operation moved by 1% of the time
where the time goes in v4:
time: 355 us
  Pallas kernels  354 us (100%)
    pallas_call x1, Pallas kernels, step(): pl.pallas_call(functools.partial(mlp_kernel, n), out_shape=pltpu.VMEM((ro...  354 us

profile of v4, /device:TPU:21, one launch (start us, length us, event | category | flops | bytes accessed | tf_op | source)
XLA Modules:
  0.0 355.3 jit_solution(552083376171550310)
XLA Ops:
  0.0 353.9 %mlp_ring.1 = bf16[224,5120]{1,0:T(8,128)(2,1)S(1)} custom-call(bf16[224,5120]{1,0:T(8,128)(2,1)} %x_hbm.1, bf16[5120,2048]{1,0:T(8,128)(2,1)} %wg_hbm.1, bf16[5120,2048]{1,0:T(8,128)(2,1)} %wu_hbm.1, bf16[2048,5120]{1,0:T(8,128)(2,1)} %wd_hbm.1), custom_call_target="tpu_custom_call" | custom-call | tf_op jit(solution)/shard_map/mlp_ring/pallas_call | solution.py:261
  353.9 1.4 copy.6

commit v5 on v4

--- a/solution.py
+++ b/solution.py
@@ -10,7 +10,7 @@
 MESH = pl.DeviceIdType.MESH
 TILE_UP = 256
 TILE_DOWN = 512
-PIECE = 1024
+PIECES = (5, 4, 1)
 DEPTH = 3
 HEAD = 48
 KEPT = 4
@@ -22,7 +22,7 @@
 def mlp_kernel(
     n, x_hbm, wg_hbm, wu_hbm, wd_hbm, y_ref,
     xbuf, hid, rbuf, wbuf, dbuf, obuf,
-    x_sem, w_sem, d_sem, send_sem, ag_recv, rs_recv,
+    w_sem, d_sem, send_sem, ag_recv, rs_recv,
 ):
     me = lax.axis_index("tp")
     peers = (lax.rem(me + 1, n), lax.rem(me + n - 1, n))
@@ -32,14 +32,15 @@
     sends = units - 1
     up_tiles = wg_hbm.shape[1] // TILE_UP
     down_tiles = width // TILE_DOWN
-    pieces = width // PIECE
+    pieces = len(PIECES)
+    starts = tuple(sum(PIECES[:p]) for p in range(pieces))
     first = (0, pieces, 0, 1, 3, pieces, 0)
-    per_piece = PIECE // TILE_DOWN
+    gather_left, sum_left = (0, 0, 1, 2, 3, 3, 3), (1, 2, 3, 3, 3, 0, 0)
     top, bottom = pl.ds(0, half), pl.ds(half, half)
 
     def x_load(h, part):
         rws = pl.ds(h * half + (0, HEAD)[part], (HEAD, half - HEAD)[part])
-        return pltpu.make_async_copy(x_hbm.at[rws], xbuf.at[0, rws], x_sem.at[h, part])
+        return pltpu.make_async_copy(x_hbm.at[rws], xbuf.at[0, rws], (w_sem, d_sem)[h].at[part])
 
     def w_load(g):
         slot = lax.rem(g, DEPTH)
@@ -58,23 +59,23 @@
         cols = pl.ds(pl.multiple_of(lax.rem(q, down_tiles) * TILE_DOWN, TILE_DOWN), TILE_DOWN)
         return pltpu.make_async_copy(wd_hbm.at[:, cols], dbuf.at[slot], d_sem.at[slot])
 
-    def gather_copy(k, d, src, dst_unit, dst_rows):
+    def gather_copy(k, d, src, dst_unit, dst_rows, sem=None):
         return pltpu.make_async_remote_copy(
             src_ref=src,
             dst_ref=xbuf.at[dst_unit, dst_rows],
-            send_sem=send_sem.at[k],
+            send_sem=send_sem.at[gather_left[k] if sem is None else sem],
             recv_sem=ag_recv.at[d, lax.rem(k, ag_recv.shape[1])],
             device_id={"tp": peers[d]},
             device_id_type=MESH,
         )
 
-    def sum_copy(r, base, d, p, src, dst):
+    def sum_copy(base, sem, d, p, src, dst):
         rws = (bottom, top)[d]
-        cols = pl.ds(0, width) if p is None else pl.ds(pl.multiple_of(p * PIECE, PIECE), PIECE)
+        cols = pl.ds(0, width) if p is None else pl.ds(starts[p] * TILE_DOWN, PIECES[p] * TILE_DOWN)
         return pltpu.make_async_remote_copy(
             src_ref=src.at[rws, cols],
             dst_ref=dst.at[rws, cols],
-            send_sem=send_sem.at[lax.rem(r + 2, sends)],
+            send_sem=send_sem.at[sem],
             recv_sem=ag_recv.at[d, base] if p is None else rs_recv.at[d, base + p],
             device_id={"tp": peers[d]},
             device_id_type=MESH,
@@ -83,11 +84,11 @@
     def landing(r):
         return rbuf.at[r] if r < KEPT else xbuf.at[r - 1]
 
-    def left(k):
+    def left(sem, blocks):
         pltpu.make_async_remote_copy(
-            src_ref=xbuf.at[0],
-            dst_ref=xbuf.at[0],
-            send_sem=send_sem.at[k],
+            src_ref=xbuf.at[pl.ds(0, blocks)],
+            dst_ref=xbuf.at[pl.ds(0, blocks)],
+            send_sem=send_sem.at[sem],
             recv_sem=ag_recv.at[0, 0],
             device_id={"tp": peers[0]},
             device_id_type=MESH,
@@ -136,11 +137,11 @@
         lax.fori_loop(0, up_tiles, tile, 0)
 
     def down(r, u, ready, finish, done):
-        def piece(p, carry):
+        for p in range(pieces):
             ready(p)
 
-            def tile(t, c2):
-                i = p * per_piece + t
+            def tile(t, carry, p=p):
+                i = starts[p] + t
                 q = r * down_tiles + i
                 d_load(q).wait()
 
@@ -149,50 +150,50 @@
                     d_load(q + DEPTH - 1).start()
 
                 term = jnp.dot(hid[u], dbuf[lax.rem(q, DEPTH)], preferred_element_type=jnp.float32)
-                finish(pl.ds(pl.multiple_of(i * TILE_DOWN, TILE_DOWN), TILE_DOWN), term)
-                return c2
-
-            lax.fori_loop(0, per_piece, tile, 0)
+                finish(pl.ds(pl.multiple_of(i * TILE_DOWN, TILE_DOWN), TILE_DOWN), term, t)
+                return carry
+
+            lax.fori_loop(0, PIECES[p], tile, 0)
             done(p)
-            return carry
-
-        lax.fori_loop(0, pieces, piece, 0)
 
     def unit(j, carry):
         @pl.when((j >= 1) & (j < sends))
         def _():
             for d in (0, 1):
-                gather_copy(j - 1, d, xbuf.at[0, (top, bottom)[d]], j, (top, bottom)[d]).wait_recv()
+                gather_copy(j - 1, d, xbuf.at[0, (top, bottom)[d]], j, (top, bottom)[d], 0).wait_recv()
 
         @pl.when(j == sends)
         def _():
             for d in (0, 1):
-                gather_copy(j - 1, d, xbuf.at[0, (bottom, top)[d]], j, (bottom, top)[d]).wait_recv()
-
-        @pl.when((j >= 1) & (j < sends - 2))
+                gather_copy(j - 1, d, xbuf.at[0, (bottom, top)[d]], j, (bottom, top)[d], 0).wait_recv()
+
+        for lo, hi in ((1, 3), (3, sends - 2)):
+
+            @pl.when((j >= lo) & (j < hi))
+            def _(lo=lo):
+                sem = j if lo == 1 else 3
+                for d in (0, 1):
+                    rws = (top, bottom)[d]
+                    gather_copy(j + 1, d, xbuf.at[j, rws], j + 2, rws, sem).start()
+
+        @pl.when(j == sends - 2)
         def _():
             for d in (0, 1):
-                rws = (top, bottom)[d]
-                gather_copy(j + 1, d, xbuf.at[j, rws], j + 2, rws).start()
-
-        @pl.when(j == sends - 2)
-        def _():
-            for d in (0, 1):
-                gather_copy(j + 1, d, xbuf.at[j, (top, bottom)[d]], j + 2, (bottom, top)[d]).start()
+                gather_copy(j + 1, d, xbuf.at[j, (top, bottom)[d]], j + 2, (bottom, top)[d], 3).start()
 
         hidden(j)
 
         @pl.when((j == sends - 2) | (j == sends))
         def _():
             r = (j - (sends - 2)) // 2
-            left(r + 2)
-
-            def finish(cols, term):
+            left(r + 1, 1)
+
+            def finish(cols, term, t):
                 xbuf[r + 1, :, cols] = term.astype(xbuf.dtype)
 
             def done(p):
                 for d in (0, 1):
-                    sum_copy(r, r * pieces, d, p, xbuf.at[r + 1], rbuf.at[r]).start()
+                    sum_copy(r * pieces, r + 1, d, p, xbuf.at[r + 1], rbuf.at[r]).start()
 
             down(r, j, nothing, finish, done)
 
@@ -200,21 +201,21 @@
 
     lax.fori_loop(0, units, unit, 0)
 
-    for k in (4, 5, 6, 0, 1):
-        left(k)
+    left(0, 2)
+    left(3, 3)
 
     def arrived(s, p):
         for d in (0, 1):
-            sum_copy(s, first[s], d, p, landing(s), landing(s)).wait_recv()
+            sum_copy(first[s], sum_left[s], d, p, landing(s), landing(s)).wait_recv()
 
     def send(r, p):
         for d in (0, 1):
-            sum_copy(r, first[r], d, p, landing(AFTER[r]), landing(r)).start()
+            sum_copy(first[r], sum_left[r], d, p, landing(AFTER[r]), landing(r)).start()
 
     for r in range(2, sends):
         s = AFTER[r]
 
-        def finish(cols, term, s=s):
+        def finish(cols, term, t, s=s):
             total = landing(s)
             total[:, cols] = (total[:, cols].astype(jnp.float32) + term).astype(total.dtype)
 
@@ -230,25 +231,26 @@
         if r not in SPLIT:
             send(r, None)
 
-    for r in range(sends - 2):
-        left((r + 2) % sends)
+    left(1, 1)
+    left(2, 1)
+    left(3, 3)
 
     early, late = landing(4), landing(6)
 
-    def finish(cols, term):
-        within = pl.ds(pl.multiple_of(lax.rem(cols.start, PIECE), TILE_DOWN), TILE_DOWN)
+    def finish(cols, term, t):
+        within = pl.ds(pl.multiple_of(t * TILE_DOWN, TILE_DOWN), TILE_DOWN)
         obuf[:, within] = term + early[:, cols].astype(jnp.float32)
 
     def done(p):
         arrived(6, p)
-        cols = pl.ds(pl.multiple_of(p * PIECE, PIECE), PIECE)
+        size = PIECES[p] * TILE_DOWN
+        cols = pl.ds(starts[p] * TILE_DOWN, size)
         for own, other in ((top, bottom), (bottom, top)):
-            y_ref[own, cols] = (obuf[own, :] + late[other, cols].astype(jnp.float32)).astype(y_ref.dtype)
+            y_ref[own, cols] = (obuf[own, pl.ds(0, size)] + late[other, cols].astype(jnp.float32)).astype(y_ref.dtype)
 
     arrived(4, None)
     down(units - 1, 0, nothing, finish, done)
-    for r in (sends - 2, sends - 1):
-        left((r + 2) % sends)
+    left(0, 2)
 
 
 def solution(mesh):
@@ -269,13 +271,12 @@
                 pltpu.VMEM((KEPT, rows, width), x.dtype),
                 pltpu.VMEM((DEPTH, width, 2 * TILE_UP), x.dtype),
                 pltpu.VMEM((DEPTH, hidden, TILE_DOWN), x.dtype),
-                pltpu.VMEM((rows, PIECE), jnp.float32),
-                pltpu.SemaphoreType.DMA((2, 2)),
+                pltpu.VMEM((rows, max(PIECES) * TILE_DOWN), jnp.float32),
                 pltpu.SemaphoreType.DMA((DEPTH,)),
                 pltpu.SemaphoreType.DMA((DEPTH,)),
-                pltpu.SemaphoreType.DMA((n - 1,)),
+                pltpu.SemaphoreType.DMA((4,)),
                 pltpu.SemaphoreType.DMA((2, n // 2)),
-                pltpu.SemaphoreType.DMA((2, 2 * (width // PIECE))),
+                pltpu.SemaphoreType.DMA((2, 2 * len(PIECES))),
             ],
             compiler_params=pltpu.CompilerParams(
                 collective_id=0, has_side_effects=True, vmem_limit_bytes=62000000

time: 355 us -> 355 us (level)
  no operation moved by 1% of the time
where the time goes in v5:
time: 355 us
  Pallas kernels  354 us (100%)
    pallas_call x1, Pallas kernels, step(): pl.pallas_call(functools.partial(mlp_kernel, n), out_shape=pltpu.VMEM((ro...  354 us

profile of v5, /device:TPU:21, one launch (start us, length us, event | category | flops | bytes accessed | tf_op | source)
XLA Modules:
  0.0 355.1 jit_solution(11017404080012778191)
XLA Ops:
  0.0 353.7 %mlp_ring.1 = bf16[224,5120]{1,0:T(8,128)(2,1)S(1)} custom-call(bf16[224,5120]{1,0:T(8,128)(2,1)} %x_hbm.1, bf16[5120,2048]{1,0:T(8,128)(2,1)} %wg_hbm.1, bf16[5120,2048]{1,0:T(8,128)(2,1)} %wu_hbm.1, bf16[2048,5120]{1,0:T(8,128)(2,1)} %wd_hbm.1), custom_call_target="tpu_custom_call" | custom-call | tf_op jit(solution)/shard_map/mlp_ring/pallas_call | solution.py:263
  353.7 1.4 copy.6

commit v6 on v5

--- a/solution.py
+++ b/solution.py
@@ -64,20 +64,20 @@
             src_ref=src,
             dst_ref=xbuf.at[dst_unit, dst_rows],
             send_sem=send_sem.at[gather_left[k] if sem is None else sem],
-            recv_sem=ag_recv.at[d, lax.rem(k, ag_recv.shape[1])],
+            recv_sem=ag_recv.at[lax.rem(k, ag_recv.shape[0])],
             device_id={"tp": peers[d]},
             device_id_type=MESH,
         )
 
     def sum_copy(base, sem, d, p, src, dst):
-        rws = (bottom, top)[d]
+        rws = (bottom, top, pl.ds(0, rows))[d]
         cols = pl.ds(0, width) if p is None else pl.ds(starts[p] * TILE_DOWN, PIECES[p] * TILE_DOWN)
         return pltpu.make_async_remote_copy(
             src_ref=src.at[rws, cols],
             dst_ref=dst.at[rws, cols],
             send_sem=send_sem.at[sem],
-            recv_sem=ag_recv.at[d, base] if p is None else rs_recv.at[d, base + p],
-            device_id={"tp": peers[d]},
+            recv_sem=ag_recv.at[base] if p is None else rs_recv.at[base + p],
+            device_id={"tp": peers[d % 2]},
             device_id_type=MESH,
         )
 
@@ -89,7 +89,7 @@
             src_ref=xbuf.at[pl.ds(0, blocks)],
             dst_ref=xbuf.at[pl.ds(0, blocks)],
             send_sem=send_sem.at[sem],
-            recv_sem=ag_recv.at[0, 0],
+            recv_sem=ag_recv.at[0],
             device_id={"tp": peers[0]},
             device_id_type=MESH,
         ).wait_send()
@@ -157,15 +157,9 @@
             done(p)
 
     def unit(j, carry):
-        @pl.when((j >= 1) & (j < sends))
+        @pl.when(j >= 1)
         def _():
-            for d in (0, 1):
-                gather_copy(j - 1, d, xbuf.at[0, (top, bottom)[d]], j, (top, bottom)[d], 0).wait_recv()
-
-        @pl.when(j == sends)
-        def _():
-            for d in (0, 1):
-                gather_copy(j - 1, d, xbuf.at[0, (bottom, top)[d]], j, (bottom, top)[d], 0).wait_recv()
+            gather_copy(j - 1, 0, xbuf.at[0], j, pl.ds(0, rows), 0).wait_recv()
 
         for lo, hi in ((1, 3), (3, sends - 2)):
 
@@ -205,8 +199,7 @@
     left(3, 3)
 
     def arrived(s, p):
-        for d in (0, 1):
-            sum_copy(first[s], sum_left[s], d, p, landing(s), landing(s)).wait_recv()
+        sum_copy(first[s], sum_left[s], 2, p, landing(s), landing(s)).wait_recv()
 
     def send(r, p):
         for d in (0, 1):
@@ -275,8 +268,8 @@
                 pltpu.SemaphoreType.DMA((DEPTH,)),
                 pltpu.SemaphoreType.DMA((DEPTH,)),
                 pltpu.SemaphoreType.DMA((4,)),
-                pltpu.SemaphoreType.DMA((2, n // 2)),
-                pltpu.SemaphoreType.DMA((2, 2 * len(PIECES))),
+                pltpu.SemaphoreType.DMA((n // 2,)),
+                pltpu.SemaphoreType.DMA((2 * len(PIECES),)),
             ],
             compiler_params=pltpu.CompilerParams(
                 collective_id=0, has_side_effects=True, vmem_limit_bytes=62000000

time: 355 us -> 355 us (level)
  no operation moved by 1% of the time
where the time goes in v6:
time: 355 us
  Pallas kernels  354 us (100%)
    pallas_call x1, Pallas kernels, step(): pl.pallas_call(functools.partial(mlp_kernel, n), out_shape=pltpu.VMEM((ro...  354 us

profile of v6, /device:TPU:21, one launch (start us, length us, event | category | flops | bytes accessed | tf_op | source)
XLA Modules:
  0.0 355.0 jit_solution(661096485462120474)
XLA Ops:
  0.0 353.6 %mlp_ring.1 = bf16[224,5120]{1,0:T(8,128)(2,1)S(1)} custom-call(bf16[224,5120]{1,0:T(8,128)(2,1)} %x_hbm.1, bf16[5120,2048]{1,0:T(8,128)(2,1)} %wg_hbm.1, bf16[5120,2048]{1,0:T(8,128)(2,1)} %wu_hbm.1, bf16[2048,5120]{1,0:T(8,128)(2,1)} %wd_hbm.1), custom_call_target="tpu_custom_call" | custom-call | tf_op jit(solution)/shard_map/mlp_ring/pallas_call | solution.py:256
  353.6 1.4 copy.6
